TPU v7x, 32 devices: a whole 2x2x4 slice. The times are simulated.
32 devices in a mesh: ctx: 16 (over z, x, core), dp: 2 (over y).
Axes of the slice: x: 2, y: 2, z: 4, core: 2. Of those that a mesh axis runs over, the one named last changes fastest.
Arguments:
- queries: bfloat16 [4096, 1024], P(('dp', 'ctx')), parts along dimension 0, may hold values from -2.5 to 2.5
- keys: bfloat16 [4096, 128], P(('dp', 'ctx')), parts along dimension 0, may hold values from -2.5 to 2.5
- values: bfloat16 [4096, 128], P(('dp', 'ctx')), parts along dimension 0, may hold values from -6 to 6
- grad_out: bfloat16 [4096, 1024], P(('dp', 'ctx')), parts along dimension 0, may hold values from -6 to 6
- pair_order: int32 [32], P('dp'), parts along dimension 0, may hold values from 0 to 15, each once
- doc_lengths: int32 [32], P('dp'), parts along dimension 0, may hold values from 1 to 512, 2048 in all
Outputs:
- attn_out: bfloat16 [4096, 1024], P(('dp', 'ctx')), parts along dimension 0
- query_grad: bfloat16 [4096, 1024], P(('dp', 'ctx')), parts along dimension 0
- key_grad: bfloat16 [4096, 128], P(('dp', 'ctx')), parts along dimension 0
- value_grad: bfloat16 [4096, 128], P(('dp', 'ctx')), parts along dimension 0
There are 2 independent parts, one for each index of `dp`. A program takes and returns all parts, laid end to end along the dimension named above; each array names one. Nothing has to cross between parts.
Inputs may be any that keep to these rules, and one draw needn't show every extreme that they name: A permutation; the device of index d along ctx holds the sequence blocks pair_order[d] and 31 - pair_order[d], of 64 tokens each, in this order. `doc_lengths`: the documents lie end to end in sequence order; the lengths sum to 2048 and the longest has exactly 512 tokens.
All inputs are finite; a program needn't handle non-finite values.
Results may differ from a plain program's by a relative error of at most 0.01.
Values may be sent and summed in bfloat16 or wider, within the bound.
A program may use at most 128 MiB of HBM per device.

v0:
```python
import jax
import jax.numpy as jnp
from jax import lax
from jax.sharding import PartitionSpec as P


def owner_pairs(shard_ids, pair_order):
    columns = jnp.arange(pair_order.shape[0], dtype=jnp.int32)
    matched = shard_ids[:, None] == columns[None, :]
    return jnp.sum(jnp.where(matched, pair_order[None, :], 0), axis=1)


def token_labels(first_row, row_count, tokens_dev, pair_order, doc_ends):
    row_ids = first_row + jnp.arange(row_count, dtype=jnp.int32)
    shard_ids = row_ids // tokens_dev
    inside = row_ids % tokens_dev
    half_rows = tokens_dev // 2
    paired = owner_pairs(shard_ids, pair_order)
    seq_block = jnp.where(inside < half_rows, paired, 2 * pair_order.shape[0] - 1 - paired)
    position = seq_block * half_rows + inside % half_rows
    document = jnp.sum((doc_ends[None, :] <= position[:, None]).astype(jnp.int32), axis=1)
    return (position, document)


def score_block(query_flat, key_rows, head_count):
    raw_scores = lax.dot_general(
        query_flat, key_rows, (((1,), (1,)), ((), ())), preferred_element_type=jnp.float32
    )
    return raw_scores.reshape(-1, head_count, key_rows.shape[0]) * key_rows.shape[1] ** (-0.5)


def block_rows(row_count, key_block):
    step_rows = min(key_block, row_count)
    while row_count % step_rows:
        step_rows = step_rows // 2
    return step_rows


def over_blocks(step_fn, carried, key_rows, value_rows, first_row, key_block):
    row_count = key_rows.shape[0]
    step_rows = block_rows(row_count, key_block)

    def one_block(block_id, current):
        begin_row = block_id * step_rows
        key_part = lax.dynamic_slice_in_dim(key_rows, begin_row, step_rows, 0)
        value_part = lax.dynamic_slice_in_dim(value_rows, begin_row, step_rows, 0)
        return step_fn(current, key_part, value_part, first_row + begin_row)

    return lax.fori_loop(0, row_count // step_rows, one_block, carried)


def shards(queries, keys, values, grad_out, pair_order, doc_lengths):
    tokens_dev = queries.shape[0]
    head_dim = keys.shape[1]
    head_count = queries.shape[1] // head_dim
    devices = lax.axis_size("ctx")
    key_block = tokens_dev * min(8, devices)
    score_scale = head_dim ** (-0.5)
    doc_ends = jnp.cumsum(doc_lengths)
    my_pos, my_doc = token_labels(
        lax.axis_index("ctx") * tokens_dev, tokens_dev, tokens_dev, pair_order, doc_ends
    )
    query_flat = queries.reshape(tokens_dev * head_count, head_dim)
    grad_flat = grad_out.reshape(tokens_dev * head_count, head_dim)

    def visible(first_row, row_count):
        key_pos, key_doc = token_labels(first_row, row_count, tokens_dev, pair_order, doc_ends)
        return (my_doc[:, None] == key_doc[None, :]) & (key_pos[None, :] <= my_pos[:, None])

    def forward_step(carried, key_rows, value_rows, first_row):
        allowed = visible(first_row, key_rows.shape[0])

        def attend(current):
            scores = score_block(query_flat, key_rows, head_count)
            exp_scores = jnp.where(allowed[:, None, :], jnp.exp(scores), 0.0)
            totals = current[0] + jnp.sum(exp_scores, axis=2)
            rounded = exp_scores.astype(jnp.bfloat16).reshape(tokens_dev * head_count, -1)
            summed = current[1] + jnp.dot(rounded, value_rows, preferred_element_type=jnp.float32)
            return (totals, summed)

        return lax.cond(jnp.any(allowed), attend, lambda current: current, carried)

    start_state = (
        jnp.zeros((tokens_dev, head_count), jnp.float32),
        jnp.zeros((tokens_dev * head_count, head_dim), jnp.float32),
    )
    all_keys, all_values = (
        lax.all_gather(keys, "ctx", axis=0, tiled=True),
        lax.all_gather(values, "ctx", axis=0, tiled=True),
    )
    totals, summed = over_blocks(forward_step, start_state, all_keys, all_values, 0, key_block)
    attn_out = (summed.reshape(tokens_dev, head_count, head_dim) / totals[:, :, None]).astype(
        jnp.bfloat16
    )
    log_totals = jnp.log(totals)
    row_dots = jnp.sum(
        grad_out.reshape(tokens_dev, head_count, head_dim).astype(jnp.float32)
        * attn_out.astype(jnp.float32),
        axis=2,
    )

    def grad_parts(key_rows, value_rows, allowed):
        scores = score_block(query_flat, key_rows, head_count)
        prob_f32 = jnp.where(allowed[:, None, :], jnp.exp(scores - log_totals[:, :, None]), 0.0)
        grad_prob = lax.dot_general(
            grad_flat, value_rows, (((1,), (1,)), ((), ())), preferred_element_type=jnp.float32
        )
        grad_prob = grad_prob.reshape(tokens_dev, head_count, -1)
        grad_score = (prob_f32 * (grad_prob - row_dots[:, :, None])).astype(jnp.bfloat16)
        prob_b = prob_f32.astype(jnp.bfloat16)
        return (
            grad_score.reshape(tokens_dev * head_count, -1),
            prob_b.reshape(tokens_dev * head_count, -1),
        )

    def key_products(grad_score, prob_b):
        key_part = lax.dot_general(
            grad_score, query_flat, (((0,), (0,)), ((), ())), preferred_element_type=jnp.float32
        )
        value_part = lax.dot_general(
            prob_b, grad_flat, (((0,), (0,)), ((), ())), preferred_element_type=jnp.float32
        )
        return jnp.concatenate([key_part, value_part], axis=1)

    query_zero = jnp.zeros((tokens_dev * head_count, head_dim), jnp.float32)

    def query_step(carried, key_rows, value_rows, first_row):
        allowed = visible(first_row, key_rows.shape[0])

        def accumulate(current):
            grad_score, prob_b = grad_parts(key_rows, value_rows, allowed)
            return current + jnp.dot(grad_score, key_rows, preferred_element_type=jnp.float32)

        return lax.cond(jnp.any(allowed), accumulate, lambda current: current, carried)

    query_sum = over_blocks(query_step, query_zero, all_keys, all_values, 0, key_block)

    def key_term(key_rows, value_rows, first_row):
        allowed = visible(first_row, key_rows.shape[0])

        def compute(current):
            grad_score, prob_b = grad_parts(key_rows, value_rows, allowed)
            return key_products(grad_score, prob_b)

        empty_term = jnp.zeros((key_rows.shape[0], 2 * head_dim), jnp.float32)
        return lax.cond(jnp.any(allowed), compute, lambda current: current, empty_term)

    key_rows = all_keys
    value_rows = all_values
    step_rows = block_rows(tokens_dev * lax.axis_size("ctx"), key_block)

    def one_part(block_id):
        begin_row = block_id * step_rows
        key_part = lax.dynamic_slice_in_dim(key_rows, begin_row, step_rows, 0)
        value_part = lax.dynamic_slice_in_dim(value_rows, begin_row, step_rows, 0)
        return key_term(key_part, value_part, begin_row)

    stacked = lax.map(
        one_part, jnp.arange(tokens_dev * lax.axis_size("ctx") // step_rows, dtype=jnp.int32)
    )
    key_sums = lax.psum_scatter(
        stacked.reshape(tokens_dev * lax.axis_size("ctx"), 2 * head_dim),
        "ctx",
        scatter_dimension=0,
        tiled=True,
    )
    query_grad = (
        (score_scale * query_sum).reshape(tokens_dev, head_count * head_dim).astype(jnp.bfloat16)
    )
    key_grad = (score_scale * key_sums[:, :head_dim]).astype(jnp.bfloat16)
    value_grad = key_sums[:, head_dim:].astype(jnp.bfloat16)
    return (attn_out.reshape(tokens_dev, head_count * head_dim), query_grad, key_grad, value_grad)


def solution(mesh):
    placed = (
        P(("dp", "ctx"), None),
        P(("dp", "ctx"), None),
        P(("dp", "ctx"), None),
        P(("dp", "ctx"), None),
        P("dp"),
        P("dp"),
    )
    return jax.shard_map(
        shards,
        mesh=mesh,
        in_specs=placed,
        out_specs=(
            P(("dp", "ctx"), None),
            P(("dp", "ctx"), None),
            P(("dp", "ctx"), None),
            P(("dp", "ctx"), None),
        ),
        check_vma=False,
    )
```

profile of v0, /device:TPU:0, one launch (start us, length us, event | category | flops | bytes accessed | tf_op | source)
XLA Modules:
  0.0 180.1 jit_solution(15258579255375141689)
XLA Ops:
  12.7 24.8 %all_gather.6 = bf16[2048,128]{1,0:T(8,128)(2,1)S(1)} all-gather(bf16[128,128]{1,0:T(8,128)(2,1)} %param.19), channel_id=1, replica_groups=mesh['ctx'=16,'dp'=2] {'ctx'}, dimensions={0}, use_global_device_ids=true | all-gather | bytes 557056 | tf_op jit(solution)/shard_map/all_gather | solution.py:88
  37.6 20.5 %all_gather.7 = bf16[2048,128]{1,0:T(8,128)(2,1)} all-gather(bf16[128,128]{1,0:T(8,128)(2,1)} %param.20), channel_id=1, replica_groups=mesh['ctx'=16,'dp'=2] {'ctx'}, dimensions={0}, use_global_device_ids=true | all-gather | bytes 557056 | tf_op jit(solution)/shard_map/all_gather | solution.py:89
  58.3 13.9 %while.50 = (s32[]{:T(128)}, f32[128,8]{1,0:T(8,128)S(1)}, f32[1024,128]{1,0:T(8,128)S(1)}, s32[128]{0:T(128)S(1)}, s32[16]{0:T(128)S(1)}, /*index=5*/s32[16]{0:...) while((s32[]{:T(128)}, f32[128,8]{1,0:T(8,128)S(1)}, ...), condition=%wide.region_10.11_spmd, body=%wide.region_3.10_spmd.sunk | while | flops 543959040 | bytes 15791513 | solution.py:49
  60.2 5.1 %conditional.6 = ((f32[128,8]{1,0:T(8,128)S(1)}, f32[1024,128]{1,0:T(8,128)S(1)})) conditional(s32[]{:T(128)} %convert_element_type.157, (f32[128,8]{1,0:T(8,128)S(1)}, f32[1024,128]{1,0:T(8,128)S(1)}) %tuple.171, (pred[128,1024]{1,0:T(8,128)(4,1)S(1)}, s32[]{:T(128)}, bf16[2048,128]{1,0:T(8,128)(2,1)S(1)}, bf16[1024,128]{1,0:T(8,128)(2,1)S(1)}, ...), branch_computations={%region_7.7_spmd, %region_8.9_spmd} | conditional | flops 543293440 | bytes 15622210 | solution.py:81
  63.0 2.1 %fusion.6 = f32[1024,128]{1,0:T(8,128)S(1)} fusion(f32[1024,128]{1,0:T(8,128)S(1)} %get-tuple-element.1071, pred[1024,1024]{0,1:T(32,128)(4,1)S(1)} %copy.21, f32[1024,1024]{1,0:T(8,128)S(1)} %get-tuple-element.1219, bf16[2048,128]{1,0:T(8,128)(2,1)} %get-tuple-element.1072, s32[]{:T(128)S(6)} %select_n.379), kind=kOutput, calls=%fused_computation.7 | convolution fusion | flops 271712256 | bytes 6553604 | tf_op jit(solution)/shard_map/while/body/eval_jaxpr/cond/branch_1_fun/dot_general | solution.py:78
  67.1 5.1 %conditional.6 = ((f32[128,8]{1,0:T(8,128)S(1)}, f32[1024,128]{1,0:T(8,128)S(1)})) conditional(s32[]{:T(128)} %convert_element_type.157, (f32[128,8]{1,0:T(8,128)S(1)}, f32[1024,128]{1,0:T(8,128)S(1)}) %tuple.171, (pred[128,1024]{1,0:T(8,128)(4,1)S(1)}, s32[]{:T(128)}, bf16[2048,128]{1,0:T(8,128)(2,1)S(1)}, bf16[1024,128]{1,0:T(8,128)(2,1)S(1)}, ...), branch_computations={%region_7.7_spmd, %region_8.9_spmd} | conditional | flops 543293440 | bytes 15622210 | solution.py:81
  69.9 2.1 %fusion.6 = f32[1024,128]{1,0:T(8,128)S(1)} fusion(f32[1024,128]{1,0:T(8,128)S(1)} %get-tuple-element.1071, pred[1024,1024]{0,1:T(32,128)(4,1)S(1)} %copy.21, f32[1024,1024]{1,0:T(8,128)S(1)} %get-tuple-element.1219, bf16[2048,128]{1,0:T(8,128)(2,1)} %get-tuple-element.1072, s32[]{:T(128)S(6)} %select_n.379), kind=kOutput, calls=%fused_computation.7 | convolution fusion | flops 271712256 | bytes 6553604 | tf_op jit(solution)/shard_map/while/body/eval_jaxpr/cond/branch_1_fun/dot_general | solution.py:78
  73.1 36.7 %while.52 = (s32[]{:T(128)}, f32[2,1024,256]{2,1,0:T(8,128)}, s32[128]{0:T(128)S(1)}, s32[16]{0:T(128)S(1)}, s32[2]{0:T(128)}, /*index=5*/s32[16]{0:T(128)S(1)},...) while((s32[]{:T(128)}, f32[2,1024,256]{2,1,0:T(8,128)}, ...), condition=%wide.region_25.26_spmd, body=%wide.region_19.25_spmd.sunk | while | flops 1085155328 | bytes 29165004 | solution.py:158
  76.8 13.2 %conditional.8 = (f32[1,1024,256]{1,2,0:T(8,128)S(1)}) conditional(s32[]{:T(128)} %convert_element_type.161, () %tuple.178, (pred[128,1024]{1,0:T(8,128)(4,1)S(1)}, s32[]{:T(128)}, bf16[2048,128]{1,0:T(8,128)(2,1)S(1)}, bf16[1024,128]{1,0:T(8,128)(2,1)S(1)}, f32[128,8]{1,0:T(8,128)S(1)}, /*index=5*/bf16[2048,128]{1,0:T(8,128)(2,1)}, ...), branch_computations={%region_23.23_spmd, %region_24.24_spmd} | conditional | flops 1084489728 | bytes 24801358 | solution.py:146
  78.7 2.6 %fusion.52 = f32[1024,1024]{1,0:T(8,128)} fusion(bf16[1024,128]{1,0:T(8,128)(2,1)S(1)} %get-tuple-element.1111, bf16[2048,128]{1,0:T(8,128)(2,1)S(1)} %get-tuple-element.1109, s32[]{:T(128)S(6)} %select_n.393), kind=kOutput, calls=%fused_computation.84 | convolution fusion | flops 268435456 | bytes 4718596 | tf_op jit(solution)/shard_map/while/body/eval_jaxpr/cond/branch_1_fun/dot_general | solution.py:26
  81.3 5.2 %fusion.49 = f32[1024,128]{0,1:T(8,128)} fusion(bf16[1024,128]{1,0:T(8,128)(2,1)S(1)} %get-tuple-element.1111, pred[1024,1024]{0,1:T(32,128)(4,1)S(1)} %copy.23, f32[1024,1024]{1,0:T(8,128)} %fusion.52, bf16[1024,128]{1,0:T(8,128)(2,1)} %get-tuple-element.1114, f32[1024]{0:T(1024)S(1)} %sub.160, f32[1024]{0:T(1024)S(1)} %sub.157, ...), kind=kOutput, calls=%fused_computation.81 | convolution fusion | flops 543162368 | bytes 6561796 | tf_op jit(solution)/shard_map/while/body/eval_jaxpr/cond/branch_1_fun/dot_general | solution.py:117
  86.5 3.5 %fusion.47 = f32[1024,128]{0,1:T(8,128)S(1)} fusion(bf16[1024,128]{1,0:T(8,128)(2,1)} %get-tuple-element.1114, pred[1024,1024]{0,1:T(32,128)(4,1)S(1)} %copy.23, f32[1024,1024]{1,0:T(8,128)} %fusion.52, f32[1024]{0:T(1024)S(1)} %sub.157), kind=kOutput, calls=%fused_computation.79 | convolution fusion | flops 272629760 | bytes 6033408 | tf_op jit(solution)/shard_map/while/body/eval_jaxpr/cond/branch_1_fun/dot_general | solution.py:120
  95.1 13.2 %conditional.8 = (f32[1,1024,256]{1,2,0:T(8,128)S(1)}) conditional(s32[]{:T(128)} %convert_element_type.161, () %tuple.178, (pred[128,1024]{1,0:T(8,128)(4,1)S(1)}, s32[]{:T(128)}, bf16[2048,128]{1,0:T(8,128)(2,1)S(1)}, bf16[1024,128]{1,0:T(8,128)(2,1)S(1)}, f32[128,8]{1,0:T(8,128)S(1)}, /*index=5*/bf16[2048,128]{1,0:T(8,128)(2,1)}, ...), branch_computations={%region_23.23_spmd, %region_24.24_spmd} | conditional | flops 1084489728 | bytes 24801358 | solution.py:146
  97.0 2.6 %fusion.52 = f32[1024,1024]{1,0:T(8,128)} fusion(bf16[1024,128]{1,0:T(8,128)(2,1)S(1)} %get-tuple-element.1111, bf16[2048,128]{1,0:T(8,128)(2,1)S(1)} %get-tuple-element.1109, s32[]{:T(128)S(6)} %select_n.393), kind=kOutput, calls=%fused_computation.84 | convolution fusion | flops 268435456 | bytes 4718596 | tf_op jit(solution)/shard_map/while/body/eval_jaxpr/cond/branch_1_fun/dot_general | solution.py:26
  99.7 5.2 %fusion.49 = f32[1024,128]{0,1:T(8,128)} fusion(bf16[1024,128]{1,0:T(8,128)(2,1)S(1)} %get-tuple-element.1111, pred[1024,1024]{0,1:T(32,128)(4,1)S(1)} %copy.23, f32[1024,1024]{1,0:T(8,128)} %fusion.52, bf16[1024,128]{1,0:T(8,128)(2,1)} %get-tuple-element.1114, f32[1024]{0:T(1024)S(1)} %sub.160, f32[1024]{0:T(1024)S(1)} %sub.157, ...), kind=kOutput, calls=%fused_computation.81 | convolution fusion | flops 543162368 | bytes 6561796 | tf_op jit(solution)/shard_map/while/body/eval_jaxpr/cond/branch_1_fun/dot_general | solution.py:117
  104.8 3.5 %fusion.47 = f32[1024,128]{0,1:T(8,128)S(1)} fusion(bf16[1024,128]{1,0:T(8,128)(2,1)} %get-tuple-element.1114, pred[1024,1024]{0,1:T(32,128)(4,1)S(1)} %copy.23, f32[1024,1024]{1,0:T(8,128)} %fusion.52, f32[1024]{0:T(1024)S(1)} %sub.157), kind=kOutput, calls=%fused_computation.79 | convolution fusion | flops 272629760 | bytes 6033408 | tf_op jit(solution)/shard_map/while/body/eval_jaxpr/cond/branch_1_fun/dot_general | solution.py:120
  110.0 21.6 %while.51 = (s32[]{:T(128)}, f32[1024,128]{1,0:T(8,128)S(1)}, s32[128]{0:T(128)S(1)}, s32[16]{0:T(128)S(1)}, s32[16]{0:T(128)S(1)}, /*index=5*/s32[128]{0:T(128)...) while((s32[]{:T(128)}, f32[1024,128]{1,0:T(8,128)S(1)}, ...), condition=%wide.region_18.19_spmd, body=%wide.region_12.18_spmd.sunk | while | flops 812394496 | bytes 15268245 | solution.py:49
  112.0 8.9 %conditional.7 = (f32[1024,128]{1,0:T(8,128)S(1)}) conditional(s32[]{:T(128)} %convert_element_type.159, f32[1024,128]{1,0:T(8,128)S(1)} %get-tuple-element.1504, (pred[128,1024]{1,0:T(8,128)(4,1)S(1)}, s32[]{:T(128)}, bf16[2048,128]{1,0:T(8,128)(2,1)S(1)}, bf16[1024,128]{1,0:T(8,128)(2,1)S(1)}, f32[128,8]{1,0:T(8,128)S(1)}, ...), branch_computations={%region_16.16_spmd, %region_17.17_spmd} | conditional | flops 811728896 | bytes 15098926 | solution.py:134
  113.9 2.6 %fusion.30 = f32[1024,1024]{1,0:T(8,128)} fusion(bf16[1024,128]{1,0:T(8,128)(2,1)S(1)} %get-tuple-element.1090, bf16[2048,128]{1,0:T(8,128)(2,1)S(1)} %get-tuple-element.1088, s32[]{:T(128)S(6)} %select_n.386), kind=kOutput, calls=%fused_computation.46 | convolution fusion | flops 268435456 | bytes 4718596 | tf_op jit(solution)/shard_map/while/body/eval_jaxpr/cond/branch_1_fun/dot_general | solution.py:26
  116.5 4.4 %fusion.26 = f32[1024,128]{1,0:T(8,128)S(1)} fusion(f32[1024,128]{1,0:T(8,128)S(1)} %get-tuple-element.1086, pred[1024,1024]{0,1:T(32,128)(4,1)S(1)} %copy.22, f32[1024,1024]{1,0:T(8,128)} %fusion.30, bf16[1024,128]{1,0:T(8,128)(2,1)} %get-tuple-element.1093, f32[1024]{0:T(1024)S(1)} %sub.151, f32[1024]{0:T(1024)S(1)} %sub.148, ...), kind=kOutput, calls=%fused_computation.43 | convolution fusion | flops 543293440 | bytes 7087104 | tf_op jit(solution)/shard_map/while/body/eval_jaxpr/cond/branch_1_fun/dot_general | solution.py:132
  122.8 8.8 %conditional.7 = (f32[1024,128]{1,0:T(8,128)S(1)}) conditional(s32[]{:T(128)} %convert_element_type.159, f32[1024,128]{1,0:T(8,128)S(1)} %get-tuple-element.1504, (pred[128,1024]{1,0:T(8,128)(4,1)S(1)}, s32[]{:T(128)}, bf16[2048,128]{1,0:T(8,128)(2,1)S(1)}, bf16[1024,128]{1,0:T(8,128)(2,1)S(1)}, f32[128,8]{1,0:T(8,128)S(1)}, ...), branch_computations={%region_16.16_spmd, %region_17.17_spmd} | conditional | flops 811728896 | bytes 15098926 | solution.py:134
  124.6 2.6 %fusion.30 = f32[1024,1024]{1,0:T(8,128)} fusion(bf16[1024,128]{1,0:T(8,128)(2,1)S(1)} %get-tuple-element.1090, bf16[2048,128]{1,0:T(8,128)(2,1)S(1)} %get-tuple-element.1088, s32[]{:T(128)S(6)} %select_n.386), kind=kOutput, calls=%fused_computation.46 | convolution fusion | flops 268435456 | bytes 4718596 | tf_op jit(solution)/shard_map/while/body/eval_jaxpr/cond/branch_1_fun/dot_general | solution.py:26
  127.3 4.3 %fusion.26 = f32[1024,128]{1,0:T(8,128)S(1)} fusion(f32[1024,128]{1,0:T(8,128)S(1)} %get-tuple-element.1086, pred[1024,1024]{0,1:T(32,128)(4,1)S(1)} %copy.22, f32[1024,1024]{1,0:T(8,128)} %fusion.30, bf16[1024,128]{1,0:T(8,128)(2,1)} %get-tuple-element.1093, f32[1024]{0:T(1024)S(1)} %sub.151, f32[1024]{0:T(1024)S(1)} %sub.148, ...), kind=kOutput, calls=%fused_computation.43 | convolution fusion | flops 543293440 | bytes 7087104 | tf_op jit(solution)/shard_map/while/body/eval_jaxpr/cond/branch_1_fun/dot_general | solution.py:132
  133.5 36.8 %reduce-scatter.2.cloned.1.call-done = f32[128,256]{1,0:T(8,128)} async-done(((f32[2048,256]{1,0:T(8,128)}), f32[128,256]{1,0:T(8,128)}) %reduce-scatter.2.cloned.1.call-update) | async-done | bytes 131088 | tf_op jit(solution)/shard_map/reduce_scatter | solution.py:161
  (101 shorter events, 36.9 us)
Async XLA Ops:
  7.2 51.1 %copy-start.3 = (s32[16]{0:T(128)S(1)}, s32[16]{0:T(128)}, u32[]{:S(2)}) copy-start(s32[16]{0:T(128)} %param.22) | copy-start | bytes 196
  7.2 163.1 %reduce-scatter.2.cloned.1.call-start = ((), (), s32[]{:S(2)}) async-start(), calls=%async_computation.1 | async-start | bytes 2228224 | tf_op jit(solution)/shard_map/reduce_scatter | solution.py:161
  72.2 0.9 copy-start.1
  86.5 3.5 %copy-start = (f32[1024,128]{0,1:T(8,128)S(1)}, f32[1024,128]{0,1:T(8,128)}, u32[]{:S(2)}) copy-start(f32[1024,128]{0,1:T(8,128)} %fusion.49) | copy-start | bytes 1572868 | tf_op jit(solution)/shard_map/while/body/eval_jaxpr/cond
  104.8 3.5 %copy-start = (f32[1024,128]{0,1:T(8,128)S(1)}, f32[1024,128]{0,1:T(8,128)}, u32[]{:S(2)}) copy-start(f32[1024,128]{0,1:T(8,128)} %fusion.49) | copy-start | bytes 1572868 | tf_op jit(solution)/shard_map/while/body/eval_jaxpr/cond
  110.0 22.5 %copy-start.2 = (f32[128,8]{1,0:T(8,128)S(1)}, f32[128,8]{1,0:T(8,128)}, u32[]{:S(2)}) copy-start(f32[128,8]{1,0:T(8,128)} %copy-done.1) | copy-start | bytes 12292
Sparse Core Ops, SparseCore 0:
  109.9 60.3 reduce-scatter.1
where the time goes:
time: 181 us; the launch traced here: 180 us
  blocking collectives  45.3 us (25%)
  matrix products  43.1 us (24%)
  waiting for transfers between devices  36.8 us (20%)
  local copies, waits for them, and re-layouts  22.9 us (13%)
  between operations  14.2 us (8%)
  other arithmetic  11.6 us (6%)
  loops' own time  6.15 us (3%)
    reduce_scatter x1, waiting for transfers between devices, shards(): lax.psum_scatter(stacked.reshape(tokens_dev * lax.axis_size('ctx'), 2 * h...  36.8 us
    all_gather x1, blocking collectives, shards(): lax.all_gather(keys, 'ctx', axis=0, tiled=True)  24.8 us
    all_gather x1, blocking collectives, shards(): lax.all_gather(values, 'ctx', axis=0, tiled=True)  20.5 us
    dot_general x6, matrix products, score_block(): lax.dot_general(query_flat, key_rows, (((1,), (1,)), ((), ())), preferred...  12.8 us
    dot_general x2, matrix products, key_products(): lax.dot_general(grad_score, query_flat, (((0,), (0,)), ((), ())), preferr...  10.3 us
    dot_general x2, matrix products, accumulate(): jnp.dot(grad_score, key_rows, preferred_element_type=jnp.float32)  8.75 us
    dot_general x2, matrix products, key_products(): lax.dot_general(prob_b, grad_flat, (((0,), (0,)), ((), ())), preferred_el...  6.92 us
    broadcast_in_dim x8, local copies, waits for them, and re-layouts, grad_parts(): jnp.where(allowed[:, None, :], jnp.exp(scores - log_totals[:, :, None]),...  6.57 us
  transfers between devices with their start and end apart: 1, of which 1 were waited for; matrix products, arithmetic and copies ran while one was open for 12% of the time, Pallas kernels for 0%

commit v1 on v0

v1 whole, which is shorter than its diff:
```python
import functools

import jax
import jax.numpy as jnp
from jax import lax
from jax.experimental import pallas as pl
from jax.experimental.pallas import tpu as pltpu
from jax.sharding import PartitionSpec as P

MESH = pl.DeviceIdType.MESH
VMEM_LIMIT = 64 * 1024 * 1024 - 128 * 1024


def flip(index, mask):
    bit = 1
    while bit <= mask:
        if mask & bit:
            index = index + bit - 2 * bit * (lax.div(index, bit) % 2)
        bit *= 2
    return index


def place(n):
    me = lax.axis_index("ctx")
    core = me % 2
    x = lax.div(me, 2) % 2
    z = lax.div(me, 4)
    return z, x, core


def index_of(z, x, core):
    return (z * 2 + x) * 2 + core


def z_order(depth):
    return sorted(range(1, depth), key=lambda mask: (-(mask & -mask), mask))


def greet(depth, z, x, core):
    barrier = pltpu.get_barrier_semaphore()
    peers = [index_of(flip(z, mask), x, core) for mask in z_order(depth)]
    peers += [index_of(z, 1 - x, core), index_of(z, x, 1 - core)]
    for peer in peers:
        pl.semaphore_signal(
            barrier, inc=1, device_id={"ctx": peer}, device_id_type=MESH
        )
    pl.semaphore_wait(barrier, len(peers))


def gather_kernel(n, k_ref, v_ref, all_ref, local_sem, zs, zr, xs, xr, cs, cr):
    depth = n // 4
    z, x, core = place(n)
    me = index_of(z, x, core)
    greet(depth, z, x, core)
    x_peer = index_of(z, 1 - x, core)
    c_peer = index_of(z, x, 1 - core)
    order = z_order(depth)
    sent = []

    def send(src, dst, send_sem, recv_sem, peer):
        copy = pltpu.make_async_remote_copy(
            src_ref=src, dst_ref=dst, send_sem=send_sem, recv_sem=recv_sem,
            device_id={"ctx": peer}, device_id_type=MESH,
        )
        copy.start()
        return copy

    def send_own(send_sem, recv_sem, peer):
        for part, ref in enumerate((k_ref, v_ref)):
            send(ref, all_ref.at[me, part], send_sem, recv_sem, peer)
        sent.append((all_ref.at[me], send_sem))

    def forward(slot, send_sem, recv_sem, peer):
        send(all_ref.at[slot], all_ref.at[slot], send_sem, recv_sem, peer)
        sent.append((all_ref.at[slot], send_sem))

    def wait_for(ref, sem):
        pltpu.make_async_copy(ref, ref, sem).wait()

    for mask in order:
        send_own(zs.at[mask], zr.at[mask], index_of(flip(z, mask), x, core))
    send_own(xs.at[0], xr.at[0], x_peer)
    send_own(cs.at[0, 0], cr.at[0, 0], c_peer)
    local = [
        pltpu.make_async_copy(ref, all_ref.at[me, part], local_sem.at[part])
        for part, ref in enumerate((k_ref, v_ref))
    ]
    for copy in local:
        copy.start()

    arrival = [0] + order[::-1]
    for mask in order[::-1]:
        slot = index_of(flip(z, mask), x, core)
        wait_for(all_ref.at[slot], zr.at[mask])
        forward(slot, xs.at[mask], xr.at[mask], x_peer)
        forward(slot, cs.at[0, mask], cr.at[0, mask], c_peer)
    for mask in arrival:
        slot = index_of(flip(z, mask), 1 - x, core)
        wait_for(all_ref.at[slot], xr.at[mask])
        forward(slot, cs.at[1, mask], cr.at[1, mask], c_peer)
    for mask in arrival:
        for side in range(2):
            slot = index_of(flip(z, mask), 1 - x if side else x, 1 - core)
            wait_for(all_ref.at[slot], cr.at[side, mask])
    for copy in local:
        copy.wait()
    for ref, sem in sent:
        wait_for(ref, sem)


def scatter_kernel(
    n, scale, part_ref, kg_ref, vg_ref, r1, r2, r3, s1, s2, cs, cr, xs, xr, zs, zr
):
    depth = n // 4
    z, x, core = place(n)
    greet(depth, z, x, core)
    head_dim = kg_ref.shape[1]
    x_peer = index_of(z, 1 - x, core)
    c_peer = index_of(z, x, 1 - core)
    order = z_order(depth) + [0]
    sent = []

    def send(src, dst, send_sem, recv_sem, peer):
        copy = pltpu.make_async_remote_copy(
            src_ref=src, dst_ref=dst, send_sem=send_sem, recv_sem=recv_sem,
            device_id={"ctx": peer}, device_id_type=MESH,
        )
        copy.start()
        sent.append(copy)
        return copy

    first, second, third = {}, {}, {}
    for side in (1, 0):
        for mask in order:
            row = flip(z, mask)
            slot = index_of(row, 1 - x if side else x, 1 - core)
            first[side, mask] = send(
                part_ref.at[slot], r1.at[side, mask],
                cs.at[side, mask], cr.at[side, mask], c_peer,
            )
    for mask in order:
        first[1, mask].wait_recv()
        mine = part_ref[index_of(flip(z, mask), 1 - x, core)].astype(jnp.float32)
        s1[mask] = (mine + r1[1, mask].astype(jnp.float32)).astype(jnp.bfloat16)
        second[mask] = send(s1.at[mask], r2.at[mask], xs.at[mask], xr.at[mask], x_peer)
    for mask in order:
        first[0, mask].wait_recv()
        second[mask].wait_recv()
        mine = part_ref[index_of(flip(z, mask), x, core)].astype(jnp.float32)
        mine = mine + r1[0, mask].astype(jnp.float32) + r2[mask].astype(jnp.float32)
        if mask:
            s2[mask] = mine.astype(jnp.bfloat16)
            third[mask] = send(
                s2.at[mask], r3.at[mask], zs.at[mask], zr.at[mask],
                index_of(flip(z, mask), x, core),
            )
        else:
            total = mine
    for mask in order[-2::-1]:
        third[mask].wait_recv()
        total = total + r3[mask].astype(jnp.float32)
    kg_ref[...] = (scale * total[:, :head_dim]).astype(kg_ref.dtype)
    vg_ref[...] = total[:, head_dim:].astype(vg_ref.dtype)
    for copy in sent:
        copy.wait_send()


def attend_kernel(
    n, heads, blocks, pair_ref, doc_ref, q_ref, g_ref, kv_ref,
    o_ref, dq_ref, part_ref, owner, k_buf, v_buf, e_buf, o_acc, dq_acc,
):
    tokens = q_ref.shape[0]
    rows = tokens // 2
    head_dim = q_ref.shape[1] // heads
    wide = heads * rows
    keys = blocks * rows
    scale = head_dim ** (-0.5)
    f32 = jnp.float32

    def put(i, carry):
        owner[pair_ref[i]] = i
        return carry

    lax.fori_loop(0, n, put, 0)
    part_ref[...] = jnp.zeros_like(part_ref)
    pair = pair_ref[lax.axis_index("ctx")]

    def locate(block):
        block = jnp.minimum(block, 2 * n - 1)
        late = block >= n
        dev = owner[jnp.where(late, 2 * n - 1 - block, block)]
        row = pl.multiple_of(jnp.where(late, rows, 0), rows)
        return dev, pl.ds(row, rows)

    def stack(ref, half):
        return jnp.concatenate(
            [
                ref[half * rows:(half + 1) * rows, h * head_dim:(h + 1) * head_dim]
                for h in range(heads)
            ],
            axis=0,
        )

    def unstack(ref, half, flat):
        for h in range(heads):
            ref[half * rows:(half + 1) * rows, h * head_dim:(h + 1) * head_dim] = flat[
                h * rows:(h + 1) * rows
            ].astype(ref.dtype)

    for half in range(2):
        block = 2 * n - 1 - pair if half else pair
        q_pos = block * rows + lax.broadcasted_iota(jnp.int32, (1, wide), 1) % rows

        def starts(i, carry):
            begin, of_rows, of_first = carry
            of_rows = jnp.where(begin <= q_pos, begin, of_rows)
            of_first = jnp.where(begin <= block * rows, begin, of_first)
            return begin + doc_ref[i], of_rows, of_first

        _, q_start, first = lax.fori_loop(
            0, doc_ref.shape[0], starts,
            (jnp.int32(0), jnp.zeros((1, wide), jnp.int32), jnp.int32(0)),
        )
        begin_block = lax.div(first, rows)
        chunks = lax.div(block - begin_block, blocks) + 1
        q_flat = stack(q_ref, half)
        g_flat = stack(g_ref, half)
        o_acc[...] = jnp.zeros_like(o_acc)
        dq_acc[...] = jnp.zeros_like(dq_acc)

        def fetch(chunk):
            for i in range(blocks):
                dev, where = locate(begin_block + chunk * blocks + i)
                k_buf[i * rows:(i + 1) * rows] = kv_ref[dev, 0, where, :]
                v_buf[i * rows:(i + 1) * rows] = kv_ref[dev, 1, where, :]
            return k_buf[...], v_buf[...]

        def forward(chunk, total):
            k, v = fetch(chunk)
            scores = lax.dot_general(
                k, q_flat, (((1,), (1,)), ((), ())), preferred_element_type=f32
            )
            k_pos = (begin_block + chunk * blocks) * rows + lax.broadcasted_iota(
                jnp.int32, (keys, 1), 0
            )
            seen = (k_pos >= q_start) & (k_pos <= q_pos)
            exp_scores = jnp.where(seen, jnp.exp(scores * scale), 0.0)
            e_buf[chunk] = exp_scores
            o_acc[...] += lax.dot_general(
                v, exp_scores.astype(jnp.bfloat16), (((0,), (0,)), ((), ())),
                preferred_element_type=f32,
            )
            return total + jnp.sum(exp_scores, axis=0, keepdims=True)

        total = lax.fori_loop(0, chunks, forward, jnp.zeros((1, wide), f32))
        inverse = 1.0 / total
        out = (o_acc[...] / total).astype(jnp.bfloat16).astype(f32)
        unstack(o_ref, half, out.T)
        row_dot = jnp.sum(g_flat.astype(f32).T * out, axis=0, keepdims=True)

        def backward(chunk, carry):
            k, v = fetch(chunk)
            prob = e_buf[chunk] * inverse
            grad_prob = lax.dot_general(
                v, g_flat, (((1,), (1,)), ((), ())), preferred_element_type=f32
            )
            grad_score = (prob * (grad_prob - row_dot)).astype(jnp.bfloat16)
            dq_acc[...] += lax.dot_general(
                k, grad_score, (((0,), (0,)), ((), ())), preferred_element_type=f32
            )
            dk = jnp.dot(grad_score, q_flat, preferred_element_type=f32)
            dv = jnp.dot(prob.astype(jnp.bfloat16), g_flat, preferred_element_type=f32)
            for i in range(blocks):
                at = begin_block + chunk * blocks + i
                dev, where = locate(at)

                @pl.when(at <= block)
                def _():
                    cut = slice(i * rows, (i + 1) * rows)
                    for side, grad in enumerate((dk, dv)):
                        cols = slice(side * head_dim, (side + 1) * head_dim)
                        old = part_ref[dev, where, cols].astype(f32)
                        part_ref[dev, where, cols] = (old + grad[cut]).astype(jnp.bfloat16)

            return carry

        lax.fori_loop(0, chunks, backward, 0)
        unstack(dq_ref, half, (scale * dq_acc[...]).T)


def shards(queries, keys, values, grad_out, pair_order, doc_lengths):
    tokens, width = queries.shape
    head_dim = keys.shape[1]
    heads = width // head_dim
    n = lax.axis_size("ctx")
    depth = n // 4
    blocks = 4
    vmem = pl.BlockSpec(memory_space=pltpu.VMEM)
    smem = pl.BlockSpec(memory_space=pltpu.SMEM)
    dma = pltpu.SemaphoreType.DMA
    bf16, f32 = jnp.bfloat16, jnp.float32

    gathered = pl.pallas_call(
        functools.partial(gather_kernel, n),
        out_shape=jax.ShapeDtypeStruct((n, 2, tokens, head_dim), bf16),
        in_specs=[vmem] * 2,
        out_specs=vmem,
        scratch_shapes=[
            dma((2,)), dma((depth,)), dma((depth,)), dma((depth,)), dma((depth,)),
            dma((2, depth)), dma((2, depth)),
        ],
        compiler_params=pltpu.CompilerParams(
            collective_id=0, has_side_effects=True, vmem_limit_bytes=VMEM_LIMIT
        ),
        name="gather",
    )(keys, values)

    rows = tokens // 2
    wide = heads * rows
    attn_out, query_grad, terms = pl.pallas_call(
        functools.partial(attend_kernel, n, heads, blocks),
        out_shape=(
            jax.ShapeDtypeStruct((tokens, width), bf16),
            jax.ShapeDtypeStruct((tokens, width), bf16),
            jax.ShapeDtypeStruct((n, tokens, 2 * head_dim), bf16),
        ),
        in_specs=[smem, smem, vmem, vmem, vmem],
        out_specs=(vmem, vmem, vmem),
        scratch_shapes=[
            pltpu.SMEM((n,), jnp.int32),
            pltpu.VMEM((blocks * rows, head_dim), bf16),
            pltpu.VMEM((blocks * rows, head_dim), bf16),
            pltpu.VMEM((2 * n // blocks, blocks * rows, wide), f32),
            pltpu.VMEM((head_dim, wide), f32),
            pltpu.VMEM((head_dim, wide), f32),
        ],
        compiler_params=pltpu.CompilerParams(vmem_limit_bytes=VMEM_LIMIT),
        name="attend",
    )(pair_order, doc_lengths, queries, grad_out, gathered)

    term = (tokens, 2 * head_dim)
    key_grad, value_grad = pl.pallas_call(
        functools.partial(scatter_kernel, n, head_dim ** (-0.5)),
        out_shape=(jax.ShapeDtypeStruct((tokens, head_dim), bf16),) * 2,
        in_specs=[vmem],
        out_specs=(vmem, vmem),
        scratch_shapes=[
            pltpu.VMEM((2, depth) + term, bf16),
            pltpu.VMEM((depth,) + term, bf16),
            pltpu.VMEM((depth,) + term, bf16),
            pltpu.VMEM((depth,) + term, bf16),
            pltpu.VMEM((depth,) + term, bf16),
            dma((2, depth)), dma((2, depth)), dma((depth,)), dma((depth,)),
            dma((depth,)), dma((depth,)),
        ],
        compiler_params=pltpu.CompilerParams(
            collective_id=1, has_side_effects=True, vmem_limit_bytes=VMEM_LIMIT
        ),
        name="scatter",
    )(terms)
    return attn_out, query_grad, key_grad, value_grad


def solution(mesh):
    tokens = P(("dp", "ctx"), None)
    return jax.shard_map(
        shards,
        mesh=mesh,
        in_specs=(tokens, tokens, tokens, tokens, P("dp"), P("dp")),
        out_specs=(tokens,) * 4,
        check_vma=False,
    )
```

time: 181 us -> 44.8 us (0.25)
  blocking collectives: 45.3 us -> 0 us
  matrix products: 43.1 us -> 0 us
  Pallas kernels: 0 us -> 41.9 us
  waiting for transfers between devices: 36.8 us -> 0 us
  local copies, waits for them, and re-layouts: 22.9 us -> 2 us
  between operations: 14.2 us -> 0.66 us
  other arithmetic: 11.6 us -> 0 us
  loops' own time: 6.15 us -> 0 us
    all_gather x2 -> x0, blocking collectives: 45.3 us -> none  [the longest x1 24.8 us: shards(): lax.all_gather(keys, 'ctx', axis=0, tiled=True)]
    dot_general x14 -> x0, matrix products: 43.1 us -> none  [the longest x6 12.8 us: score_block(): lax.dot_general(query_flat, key_rows, (((1,), (1,)), ((), ())), preferred...]
    pallas_call x0 -> x3, Pallas kernels: none -> 41.9 us  [the longest x1 19.3 us: shards(): pl.pallas_call(functools.partial(gather_kernel, n), out_shape=jax.ShapeDt...]
    reduce_scatter x1 -> x0, waiting for transfers between devices: 36.8 us -> none  [shards(): lax.psum_scatter(stacked.reshape(tokens_dev * lax.axis_size('ctx'), 2 * h...]
    broadcast_in_dim x13 -> x0, local copies, waits for them, and re-layouts: 9.86 us -> none  [the longest x8 6.57 us: grad_parts(): jnp.where(allowed[:, None, :], jnp.exp(scores - log_totals[:, :, None]),...]
    another operation x9 -> x0, loops' own time: 6.15 us -> none  [the longest x2 3.13 us: over_blocks(): return lax.fori_loop(0, row_count // step_rows, one_block, carried)]
    reduce_or x6 -> x0, other arithmetic: 5.52 us -> none  [the longest x2 1.84 us: forward_step(): return lax.cond(jnp.any(allowed), attend, lambda current: current, carried)]
    reshape x3 -> x0, local copies, waits for them, and re-layouts: 2.92 us -> none  [the longest x1 1.77 us: shards(): grad_flat = grad_out.reshape(tokens_dev * head_count, head_dim)]
  transfers between devices with their start and end apart: 1 -> 0, of which waited for: 1 -> 0; matrix products, arithmetic and copies ran while one was open for 12% -> 0% of each run, Pallas kernels for 0% -> 0%
where the time goes in v1:
time: 44.8 us; the launch traced here: 44.6 us
  Pallas kernels  41.9 us (94%)
  local copies, waits for them, and re-layouts  2 us (4%)
  between operations  0.66 us (1%)
    pallas_call x1, Pallas kernels, shards(): pl.pallas_call(functools.partial(gather_kernel, n), out_shape=jax.ShapeDt...  19.3 us
    pallas_call x1, Pallas kernels, shards(): pl.pallas_call(functools.partial(scatter_kernel, n, head_dim ** (-0.5)),...  17 us
    pallas_call x1, Pallas kernels, shards(): pl.pallas_call(functools.partial(attend_kernel, n, heads, blocks), out_sh...  5.62 us
    unnamed x4, local copies, waits for them, and re-layouts  2 us

profile of v1, /device:TPU:0, one launch (start us, length us, event | category | flops | bytes accessed | tf_op | source)
XLA Modules:
  0.0 44.6 jit_solution(773848742357379406)
XLA Ops:
  0.6 19.3 %gather.1.kv_ref = bf16[16,2,128,128]{3,2,1,0:T(8,128)(2,1)} custom-call(bf16[128,128]{1,0:T(8,128)(2,1)} %k_ref.1, bf16[128,128]{1,0:T(8,128)(2,1)} %v_ref.1), custom_call_target="tpu_custom_call" | custom-call | tf_op jit(solution)/shard_map/gather/pallas_call | solution.py:303
  20.0 5.6 %attend.1 = (bf16[128,1024]{1,0:T(8,128)(2,1)}, bf16[128,1024]{1,0:T(8,128)(2,1)}, bf16[16,128,256]{2,1,0:T(8,128)(2,1)}) custom-call(s32[16]{0:T(128)} %pair_ref.1, s32[16]{0:T(128)} %doc_ref.1, bf16[128,1024]{1,0:T(8,128)(2,1)} %q_ref.1, bf16[128,1024]{1,0:T(8,128)(2,1)} %g_ref.1, bf16[16,2,128,128]{3,2,1,0:T(8,128)(2,1)} %gather.1.kv_ref), custom_call_target="tpu_custom_call" | custom-call | tf_op jit(solution)/shard_map/attend/pallas_call | solution.py:320
  25.6 17.0 %scatter.1 = (bf16[128,128]{1,0:T(8,128)(2,1)}, bf16[128,128]{1,0:T(8,128)(2,1)}) custom-call(bf16[16,128,256]{2,1,0:T(8,128)(2,1)} %get-tuple-element.11.part_ref), custom_call_target="tpu_custom_call" | custom-call | tf_op jit(solution)/shard_map/scatter/pallas_call | solution.py:342
  42.6 0.0 copy-start
  42.6 1.4 %copy.12 = bf16[128,128]{1,0:T(8,128)(2,1)} copy(bf16[128,128]{1,0:T(8,128)(2,1)} %get-tuple-element.20) | data formatting | bytes 65536
  44.0 0.0 copy-done
  44.0 0.6 %copy.13 = bf16[128,128]{1,0:T(8,128)(2,1)} copy(bf16[128,128]{1,0:T(8,128)(2,1)S(1)} %copy-done) | data formatting | bytes 65536
Async XLA Ops:
  42.6 1.4 %copy-start = (bf16[128,128]{1,0:T(8,128)(2,1)S(1)}, bf16[128,128]{1,0:T(8,128)(2,1)}, u32[]{:S(2)}) copy-start(bf16[128,128]{1,0:T(8,128)(2,1)} %get-tuple-element.21) | copy-start | bytes 98308

commit v2 on v1

--- a/solution.py
+++ b/solution.py
@@ -33,7 +33,7 @@
 
 
 def z_order(depth):
-    return sorted(range(1, depth), key=lambda mask: (-(mask & -mask), mask))
+    return list(range(1, depth))
 
 
 def greet(depth, z, x, core):
@@ -67,19 +67,24 @@
 
     def send_own(send_sem, recv_sem, peer):
         for part, ref in enumerate((k_ref, v_ref)):
-            send(ref, all_ref.at[me, part], send_sem, recv_sem, peer)
-        sent.append((all_ref.at[me], send_sem))
-
-    def forward(slot, send_sem, recv_sem, peer):
-        send(all_ref.at[slot], all_ref.at[slot], send_sem, recv_sem, peer)
-        sent.append((all_ref.at[slot], send_sem))
+            dst = all_ref.at[me, part]
+            send(ref, dst, send_sem.at[part], recv_sem.at[part], peer)
+            sent.append((dst, send_sem.at[part]))
 
     def wait_for(ref, sem):
         pltpu.make_async_copy(ref, ref, sem).wait()
 
+    def pass_on(slot, arrived, routes):
+        for part in range(2):
+            ref = all_ref.at[slot, part]
+            wait_for(ref, arrived.at[part])
+            for send_sem, recv_sem, peer in routes:
+                send(ref, ref, send_sem.at[part], recv_sem.at[part], peer)
+                sent.append((ref, send_sem.at[part]))
+
+    send_own(xs.at[0], xr.at[0], x_peer)
     for mask in order:
         send_own(zs.at[mask], zr.at[mask], index_of(flip(z, mask), x, core))
-    send_own(xs.at[0], xr.at[0], x_peer)
     send_own(cs.at[0, 0], cr.at[0, 0], c_peer)
     local = [
         pltpu.make_async_copy(ref, all_ref.at[me, part], local_sem.at[part])
@@ -88,20 +93,30 @@
     for copy in local:
         copy.start()
 
-    arrival = [0] + order[::-1]
-    for mask in order[::-1]:
-        slot = index_of(flip(z, mask), x, core)
-        wait_for(all_ref.at[slot], zr.at[mask])
-        forward(slot, xs.at[mask], xr.at[mask], x_peer)
-        forward(slot, cs.at[0, mask], cr.at[0, mask], c_peer)
-    for mask in arrival:
-        slot = index_of(flip(z, mask), 1 - x, core)
-        wait_for(all_ref.at[slot], xr.at[mask])
-        forward(slot, cs.at[1, mask], cr.at[1, mask], c_peer)
-    for mask in arrival:
+    def from_z(mask):
+        pass_on(
+            index_of(flip(z, mask), x, core), zr.at[mask],
+            [(xs.at[mask], xr.at[mask], x_peer), (cs.at[0, mask], cr.at[0, mask], c_peer)],
+        )
+
+    def from_x(mask):
+        pass_on(
+            index_of(flip(z, mask), 1 - x, core), xr.at[mask],
+            [(cs.at[1, mask], cr.at[1, mask], c_peer)],
+        )
+
+    for mask in order:
+        from_z(mask)
+        if mask == 1:
+            from_x(0)
+    if depth == 1:
+        from_x(0)
+    for mask in order:
+        from_x(mask)
+    for mask in [0] + order:
         for side in range(2):
             slot = index_of(flip(z, mask), 1 - x if side else x, 1 - core)
-            wait_for(all_ref.at[slot], cr.at[side, mask])
+            pass_on(slot, cr.at[side, mask], [])
     for copy in local:
         copy.wait()
     for ref, sem in sent:
@@ -114,10 +129,9 @@
     depth = n // 4
     z, x, core = place(n)
     greet(depth, z, x, core)
-    head_dim = kg_ref.shape[1]
     x_peer = index_of(z, 1 - x, core)
     c_peer = index_of(z, x, 1 - core)
-    order = z_order(depth) + [0]
+    order = z_order(depth)[::-1] + [0]
     sent = []
 
     def send(src, dst, send_sem, recv_sem, peer):
@@ -140,27 +154,37 @@
             )
     for mask in order:
         first[1, mask].wait_recv()
-        mine = part_ref[index_of(flip(z, mask), 1 - x, core)].astype(jnp.float32)
-        s1[mask] = (mine + r1[1, mask].astype(jnp.float32)).astype(jnp.bfloat16)
-        second[mask] = send(s1.at[mask], r2.at[mask], xs.at[mask], xr.at[mask], x_peer)
+        for part in range(2):
+            mine = part_ref[index_of(flip(z, mask), 1 - x, core), part].astype(jnp.float32)
+            mine = mine + r1[1, mask, part].astype(jnp.float32)
+            s1[mask, part] = mine.astype(jnp.bfloat16)
+            second[mask, part] = send(
+                s1.at[mask, part], r2.at[mask, part],
+                xs.at[mask, part], xr.at[mask, part], x_peer,
+            )
+    total = [None, None]
     for mask in order:
         first[0, mask].wait_recv()
-        second[mask].wait_recv()
-        mine = part_ref[index_of(flip(z, mask), x, core)].astype(jnp.float32)
-        mine = mine + r1[0, mask].astype(jnp.float32) + r2[mask].astype(jnp.float32)
-        if mask:
-            s2[mask] = mine.astype(jnp.bfloat16)
-            third[mask] = send(
-                s2.at[mask], r3.at[mask], zs.at[mask], zr.at[mask],
-                index_of(flip(z, mask), x, core),
-            )
-        else:
-            total = mine
-    for mask in order[-2::-1]:
-        third[mask].wait_recv()
-        total = total + r3[mask].astype(jnp.float32)
-    kg_ref[...] = (scale * total[:, :head_dim]).astype(kg_ref.dtype)
-    vg_ref[...] = total[:, head_dim:].astype(vg_ref.dtype)
+        for part in range(2):
+            mine = part_ref[index_of(flip(z, mask), x, core), part].astype(jnp.float32)
+            mine = mine + r1[0, mask, part].astype(jnp.float32)
+            second[mask, part].wait_recv()
+            mine = mine + r2[mask, part].astype(jnp.float32)
+            if mask:
+                s2[mask, part] = mine.astype(jnp.bfloat16)
+                third[mask, part] = send(
+                    s2.at[mask, part], r3.at[mask, part],
+                    zs.at[mask, part], zr.at[mask, part],
+                    index_of(flip(z, mask), x, core),
+                )
+            else:
+                total[part] = mine
+    for mask in order[:-1]:
+        for part in range(2):
+            third[mask, part].wait_recv()
+            total[part] = total[part] + r3[mask, part].astype(jnp.float32)
+    kg_ref[...] = (scale * total[0]).astype(kg_ref.dtype)
+    vg_ref[...] = total[1].astype(vg_ref.dtype)
     for copy in sent:
         copy.wait_send()
 
@@ -278,9 +302,8 @@
                 def _():
                     cut = slice(i * rows, (i + 1) * rows)
                     for side, grad in enumerate((dk, dv)):
-                        cols = slice(side * head_dim, (side + 1) * head_dim)
-                        old = part_ref[dev, where, cols].astype(f32)
-                        part_ref[dev, where, cols] = (old + grad[cut]).astype(jnp.bfloat16)
+                        old = part_ref[dev, side, where, :].astype(f32)
+                        part_ref[dev, side, where, :] = (old + grad[cut]).astype(jnp.bfloat16)
 
             return carry
 
@@ -306,8 +329,8 @@
         in_specs=[vmem] * 2,
         out_specs=vmem,
         scratch_shapes=[
-            dma((2,)), dma((depth,)), dma((depth,)), dma((depth,)), dma((depth,)),
-            dma((2, depth)), dma((2, depth)),
+            dma((2,)), dma((depth, 2)), dma((depth, 2)), dma((depth, 2)), dma((depth, 2)),
+            dma((2, depth, 2)), dma((2, depth, 2)),
         ],
         compiler_params=pltpu.CompilerParams(
             collective_id=0, has_side_effects=True, vmem_limit_bytes=VMEM_LIMIT
@@ -322,7 +345,7 @@
         out_shape=(
             jax.ShapeDtypeStruct((tokens, width), bf16),
             jax.ShapeDtypeStruct((tokens, width), bf16),
-            jax.ShapeDtypeStruct((n, tokens, 2 * head_dim), bf16),
+            jax.ShapeDtypeStruct((n, 2, tokens, head_dim), bf16),
         ),
         in_specs=[smem, smem, vmem, vmem, vmem],
         out_specs=(vmem, vmem, vmem),
@@ -338,7 +361,7 @@
         name="attend",
     )(pair_order, doc_lengths, queries, grad_out, gathered)
 
-    term = (tokens, 2 * head_dim)
+    term = (2, tokens, head_dim)
     key_grad, value_grad = pl.pallas_call(
         functools.partial(scatter_kernel, n, head_dim ** (-0.5)),
         out_shape=(jax.ShapeDtypeStruct((tokens, head_dim), bf16),) * 2,
@@ -350,8 +373,8 @@
             pltpu.VMEM((depth,) + term, bf16),
             pltpu.VMEM((depth,) + term, bf16),
             pltpu.VMEM((depth,) + term, bf16),
-            dma((2, depth)), dma((2, depth)), dma((depth,)), dma((depth,)),
-            dma((depth,)), dma((depth,)),
+            dma((2, depth)), dma((2, depth)), dma((depth, 2)), dma((depth, 2)),
+            dma((depth, 2)), dma((depth, 2)),
         ],
         compiler_params=pltpu.CompilerParams(
             collective_id=1, has_side_effects=True, vmem_limit_bytes=VMEM_LIMIT

time: 44.8 us -> 43.1 us (0.962); the launches traced: 44.6 us -> 43.5 us
  Pallas kernels: 41.9 us -> 40.8 us
    pallas_call x1, Pallas kernels: 19.3 us -> 18.3 us  [shards(): pl.pallas_call(functools.partial(gather_kernel, n), out_shape=jax.ShapeDt...]
where the time goes in v2:
time: 43.1 us; the launch traced here: 43.5 us
  Pallas kernels  40.8 us (95%)
  local copies, waits for them, and re-layouts  2 us (5%)
  between operations  0.66 us (2%)
    pallas_call x1, Pallas kernels, shards(): pl.pallas_call(functools.partial(gather_kernel, n), out_shape=jax.ShapeDt...  18.3 us
    pallas_call x1, Pallas kernels, shards(): pl.pallas_call(functools.partial(scatter_kernel, n, head_dim ** (-0.5)),...  16.8 us
    pallas_call x1, Pallas kernels, shards(): pl.pallas_call(functools.partial(attend_kernel, n, heads, blocks), out_sh...  5.7 us
    unnamed x4, local copies, waits for them, and re-layouts  2 us

profile of v2, /device:TPU:0, one launch (start us, length us, event | category | flops | bytes accessed | tf_op | source)
XLA Modules:
  0.0 43.5 jit_solution(2255491699786118179)
XLA Ops:
  0.6 18.3 %gather.1.kv_ref = bf16[16,2,128,128]{3,2,1,0:T(8,128)(2,1)} custom-call(bf16[128,128]{1,0:T(8,128)(2,1)} %k_ref.1, bf16[128,128]{1,0:T(8,128)(2,1)} %v_ref.1), custom_call_target="tpu_custom_call" | custom-call | tf_op jit(solution)/shard_map/gather/pallas_call | solution.py:326
  18.9 5.7 %attend.1 = (bf16[128,1024]{1,0:T(8,128)(2,1)}, bf16[128,1024]{1,0:T(8,128)(2,1)}, bf16[16,2,128,128]{3,2,1,0:T(8,128)(2,1)}) custom-call(s32[16]{0:T(128)} %pair_ref.1, s32[16]{0:T(128)} %doc_ref.1, bf16[128,1024]{1,0:T(8,128)(2,1)} %q_ref.1, bf16[128,1024]{1,0:T(8,128)(2,1)} %g_ref.1, bf16[16,2,128,128]{3,2,1,0:T(8,128)(2,1)} %gather.1.kv_ref), custom_call_target="tpu_custom_call" | custom-call | tf_op jit(solution)/shard_map/attend/pallas_call | solution.py:343
  24.6 16.8 %scatter.1 = (bf16[128,128]{1,0:T(8,128)(2,1)}, bf16[128,128]{1,0:T(8,128)(2,1)}) custom-call(bf16[16,2,128,128]{3,2,1,0:T(8,128)(2,1)} %get-tuple-element.11.part_ref), custom_call_target="tpu_custom_call" | custom-call | tf_op jit(solution)/shard_map/scatter/pallas_call | solution.py:365
  41.5 0.0 copy-start
  41.5 1.4 %copy.12 = bf16[128,128]{1,0:T(8,128)(2,1)} copy(bf16[128,128]{1,0:T(8,128)(2,1)} %get-tuple-element.20) | data formatting | bytes 65536
  42.8 0.0 copy-done
  42.8 0.6 %copy.13 = bf16[128,128]{1,0:T(8,128)(2,1)} copy(bf16[128,128]{1,0:T(8,128)(2,1)S(1)} %copy-done) | data formatting | bytes 65536
Async XLA Ops:
  41.5 1.4 %copy-start = (bf16[128,128]{1,0:T(8,128)(2,1)S(1)}, bf16[128,128]{1,0:T(8,128)(2,1)}, u32[]{:S(2)}) copy-start(bf16[128,128]{1,0:T(8,128)(2,1)} %get-tuple-element.21) | copy-start | bytes 98308

commit v3 on v2

--- a/solution.py
+++ b/solution.py
@@ -8,7 +8,7 @@
 from jax.sharding import PartitionSpec as P
 
 MESH = pl.DeviceIdType.MESH
-VMEM_LIMIT = 64 * 1024 * 1024 - 128 * 1024
+MIB = 1024 * 1024
 
 
 def flip(index, mask):
@@ -325,7 +325,7 @@
 
     gathered = pl.pallas_call(
         functools.partial(gather_kernel, n),
-        out_shape=jax.ShapeDtypeStruct((n, 2, tokens, head_dim), bf16),
+        out_shape=pltpu.VMEM((n, 2, tokens, head_dim), bf16),
         in_specs=[vmem] * 2,
         out_specs=vmem,
         scratch_shapes=[
@@ -333,19 +333,21 @@
             dma((2, depth, 2)), dma((2, depth, 2)),
         ],
         compiler_params=pltpu.CompilerParams(
-            collective_id=0, has_side_effects=True, vmem_limit_bytes=VMEM_LIMIT
+            collective_id=0, has_side_effects=True, vmem_limit_bytes=2 * MIB
         ),
         name="gather",
     )(keys, values)
 
     rows = tokens // 2
     wide = heads * rows
+    chunks = pl.cdiv(n // 2 + 1, blocks)
+    exp_bytes = 4 * chunks * blocks * rows * wide
     attn_out, query_grad, terms = pl.pallas_call(
         functools.partial(attend_kernel, n, heads, blocks),
         out_shape=(
             jax.ShapeDtypeStruct((tokens, width), bf16),
             jax.ShapeDtypeStruct((tokens, width), bf16),
-            jax.ShapeDtypeStruct((n, 2, tokens, head_dim), bf16),
+            pltpu.VMEM((n, 2, tokens, head_dim), bf16),
         ),
         in_specs=[smem, smem, vmem, vmem, vmem],
         out_specs=(vmem, vmem, vmem),
@@ -353,18 +355,18 @@
             pltpu.SMEM((n,), jnp.int32),
             pltpu.VMEM((blocks * rows, head_dim), bf16),
             pltpu.VMEM((blocks * rows, head_dim), bf16),
-            pltpu.VMEM((2 * n // blocks, blocks * rows, wide), f32),
+            pltpu.VMEM((chunks, blocks * rows, wide), f32),
             pltpu.VMEM((head_dim, wide), f32),
             pltpu.VMEM((head_dim, wide), f32),
         ],
-        compiler_params=pltpu.CompilerParams(vmem_limit_bytes=VMEM_LIMIT),
+        compiler_params=pltpu.CompilerParams(vmem_limit_bytes=exp_bytes + 10 * MIB),
         name="attend",
     )(pair_order, doc_lengths, queries, grad_out, gathered)
 
     term = (2, tokens, head_dim)
     key_grad, value_grad = pl.pallas_call(
         functools.partial(scatter_kernel, n, head_dim ** (-0.5)),
-        out_shape=(jax.ShapeDtypeStruct((tokens, head_dim), bf16),) * 2,
+        out_shape=(pltpu.VMEM((tokens, head_dim), bf16),) * 2,
         in_specs=[vmem],
         out_specs=(vmem, vmem),
         scratch_shapes=[
@@ -377,7 +379,8 @@
             dma((depth, 2)), dma((depth, 2)),
         ],
         compiler_params=pltpu.CompilerParams(
-            collective_id=1, has_side_effects=True, vmem_limit_bytes=VMEM_LIMIT
+            collective_id=1, has_side_effects=True,
+            vmem_limit_bytes=6 * depth * 4 * tokens * head_dim + 2 * MIB,
         ),
         name="scatter",
     )(terms)

time: 43.1 us -> 39 us (0.905); the launches traced: 43.5 us -> 38.3 us
  Pallas kernels: 40.8 us -> 34.8 us
  local copies, waits for them, and re-layouts: 2 us -> 2.8 us
    pallas_call x1, Pallas kernels: 16.8 us -> 13.8 us  [shards(): pl.pallas_call(functools.partial(scatter_kernel, n, head_dim ** (-0.5)),...]
    pallas_call x1, Pallas kernels: 18.3 us -> 16.5 us  [shards(): pl.pallas_call(functools.partial(gather_kernel, n), out_shape=pltpu.VMEM(...]
    pallas_call x1, Pallas kernels: 5.7 us -> 4.46 us  [shards(): pl.pallas_call(functools.partial(attend_kernel, n, heads, blocks), out_sh...]
    unnamed x4 -> x14, local copies, waits for them, and re-layouts: 2 us -> 2.8 us
where the time goes in v3:
time: 39 us; the launch traced here: 38.3 us
  Pallas kernels  34.8 us (89%)
  local copies, waits for them, and re-layouts  2.8 us (7%)
  between operations  0.7 us (2%)
    pallas_call x1, Pallas kernels, shards(): pl.pallas_call(functools.partial(gather_kernel, n), out_shape=pltpu.VMEM(...  16.5 us
    pallas_call x1, Pallas kernels, shards(): pl.pallas_call(functools.partial(scatter_kernel, n, head_dim ** (-0.5)),...  13.8 us
    pallas_call x1, Pallas kernels, shards(): pl.pallas_call(functools.partial(attend_kernel, n, heads, blocks), out_sh...  4.46 us
    unnamed x14, local copies, waits for them, and re-layouts  2.8 us

profile of v3, /device:TPU:0, one launch (start us, length us, event | category | flops | bytes accessed | tf_op | source)
XLA Modules:
  0.0 38.3 jit_solution(9702309177011162387)
XLA Ops:
  0.6 0.0 copy-start.1
  0.6 0.0 copy-start.2
  0.7 0.8 %copy-done.2 = bf16[128,128]{1,0:T(8,128)(2,1)S(1)} copy-done((bf16[128,128]{1,0:T(8,128)(2,1)S(1)}, bf16[128,128]{1,0:T(8,128)(2,1)}, u32[]{:S(2)}) %copy-start.2) | copy-done | bytes 32792
  1.4 0.0 copy-start.3
  1.4 0.8 %copy-done.3 = bf16[128,128]{1,0:T(8,128)(2,1)S(1)} copy-done((bf16[128,128]{1,0:T(8,128)(2,1)S(1)}, bf16[128,128]{1,0:T(8,128)(2,1)}, u32[]{:S(2)}) %copy-start.3) | copy-done | bytes 32792
  2.2 0.0 copy-start
  2.2 0.0 copy-start.4
  2.2 0.0 copy-start.5
  2.2 16.5 %gather.1.kv_ref = bf16[16,2,128,128]{3,2,1,0:T(8,128)(2,1)S(1)} custom-call(bf16[128,128]{1,0:T(8,128)(2,1)S(1)} %copy-done.2, bf16[128,128]{1,0:T(8,128)(2,1)S(1)} %copy-done.3), custom_call_target="tpu_custom_call" | custom-call | tf_op jit(solution)/shard_map/gather/pallas_call | solution.py:326
  18.7 0.0 copy-done.1
  18.7 0.0 copy-done
  18.7 0.0 copy-done.4
  18.7 0.0 copy-done.5
  18.7 4.5 %attend.1 = (bf16[128,1024]{1,0:T(8,128)(2,1)}, bf16[128,1024]{1,0:T(8,128)(2,1)}, bf16[16,2,128,128]{3,2,1,0:T(8,128)(2,1)S(1)}) custom-call(s32[16]{0:T(128)S(1)} %copy-done.4, s32[16]{0:T(128)S(1)} %copy-done.5, bf16[128,1024]{1,0:T(8,128)(2,1)S(1)} %copy-done, bf16[128,1024]{1,0:T(8,128)(2,1)S(1)} %copy-done.1, bf16[16,2,128,128]{3,2,1,0:T(8,128)(2,1)S(1)} %gather.1.kv_ref), custom_call_target="tpu_custom_call" | custom-call | tf_op jit(solution)/shard_map/attend/pallas_call | solution.py:345
  23.2 13.8 %scatter.1 = (bf16[128,128]{1,0:T(8,128)(2,1)S(1)}, bf16[128,128]{1,0:T(8,128)(2,1)S(1)}) custom-call(bf16[16,2,128,128]{3,2,1,0:T(8,128)(2,1)S(1)} %get-tuple-element.11.part_ref), custom_call_target="tpu_custom_call" | custom-call | tf_op jit(solution)/shard_map/scatter/pallas_call | solution.py:367
  37.0 0.6 %copy.12 = bf16[128,128]{1,0:T(8,128)(2,1)} copy(bf16[128,128]{1,0:T(8,128)(2,1)S(1)} %get-tuple-element.16) | data formatting | bytes 65536
  37.7 0.6 %copy.13 = bf16[128,128]{1,0:T(8,128)(2,1)} copy(bf16[128,128]{1,0:T(8,128)(2,1)S(1)} %get-tuple-element.17) | data formatting | bytes 65536
Async XLA Ops:
  0.6 18.1 %copy-start.1 = (bf16[128,1024]{1,0:T(8,128)(2,1)S(1)}, bf16[128,1024]{1,0:T(8,128)(2,1)}, u32[]{:S(2)}) copy-start(bf16[128,1024]{1,0:T(8,128)(2,1)} %g_ref.1) | copy-start | bytes 786436
  0.6 0.8 %copy-start.2 = (bf16[128,128]{1,0:T(8,128)(2,1)S(1)}, bf16[128,128]{1,0:T(8,128)(2,1)}, u32[]{:S(2)}) copy-start(bf16[128,128]{1,0:T(8,128)(2,1)} %k_ref.1) | copy-start | bytes 98308
  1.4 0.8 %copy-start.3 = (bf16[128,128]{1,0:T(8,128)(2,1)S(1)}, bf16[128,128]{1,0:T(8,128)(2,1)}, u32[]{:S(2)}) copy-start(bf16[128,128]{1,0:T(8,128)(2,1)} %v_ref.1) | copy-start | bytes 98308
  2.2 16.5 %copy-start = (bf16[128,1024]{1,0:T(8,128)(2,1)S(1)}, bf16[128,1024]{1,0:T(8,128)(2,1)}, u32[]{:S(2)}) copy-start(bf16[128,1024]{1,0:T(8,128)(2,1)} %q_ref.1) | copy-start | bytes 786436
  2.2 16.5 %copy-start.4 = (s32[16]{0:T(128)S(1)}, s32[16]{0:T(128)}, u32[]{:S(2)}) copy-start(s32[16]{0:T(128)} %pair_ref.1) | copy-start | bytes 196
  2.2 16.5 %copy-start.5 = (s32[16]{0:T(128)S(1)}, s32[16]{0:T(128)}, u32[]{:S(2)}) copy-start(s32[16]{0:T(128)} %doc_ref.1) | copy-start | bytes 196

commit v4 on v3

--- a/solution.py
+++ b/solution.py
@@ -51,7 +51,15 @@
     depth = n // 4
     z, x, core = place(n)
     me = index_of(z, x, core)
+    local = [
+        pltpu.make_async_copy(ref, all_ref.at[me, part], local_sem.at[part])
+        for part, ref in enumerate((k_ref, v_ref))
+    ]
+    for copy in local:
+        copy.start()
     greet(depth, z, x, core)
+    for copy in local:
+        copy.wait()
     x_peer = index_of(z, 1 - x, core)
     c_peer = index_of(z, x, 1 - core)
     order = z_order(depth)
@@ -66,10 +74,10 @@
         return copy
 
     def send_own(send_sem, recv_sem, peer):
-        for part, ref in enumerate((k_ref, v_ref)):
-            dst = all_ref.at[me, part]
-            send(ref, dst, send_sem.at[part], recv_sem.at[part], peer)
-            sent.append((dst, send_sem.at[part]))
+        for part in range(2):
+            ref = all_ref.at[me, part]
+            send(ref, ref, send_sem.at[part], recv_sem.at[part], peer)
+            sent.append((ref, send_sem.at[part]))
 
     def wait_for(ref, sem):
         pltpu.make_async_copy(ref, ref, sem).wait()
@@ -86,13 +94,6 @@
     for mask in order:
         send_own(zs.at[mask], zr.at[mask], index_of(flip(z, mask), x, core))
     send_own(cs.at[0, 0], cr.at[0, 0], c_peer)
-    local = [
-        pltpu.make_async_copy(ref, all_ref.at[me, part], local_sem.at[part])
-        for part, ref in enumerate((k_ref, v_ref))
-    ]
-    for copy in local:
-        copy.start()
-
     def from_z(mask):
         pass_on(
             index_of(flip(z, mask), x, core), zr.at[mask],
@@ -117,8 +118,6 @@
         for side in range(2):
             slot = index_of(flip(z, mask), 1 - x if side else x, 1 - core)
             pass_on(slot, cr.at[side, mask], [])
-    for copy in local:
-        copy.wait()
     for ref, sem in sent:
         wait_for(ref, sem)
 
@@ -326,7 +325,7 @@
     gathered = pl.pallas_call(
         functools.partial(gather_kernel, n),
         out_shape=pltpu.VMEM((n, 2, tokens, head_dim), bf16),
-        in_specs=[vmem] * 2,
+        in_specs=[pl.BlockSpec(memory_space=pltpu.HBM)] * 2,
         out_specs=vmem,
         scratch_shapes=[
             dma((2,)), dma((depth, 2)), dma((depth, 2)), dma((depth, 2)), dma((depth, 2)),
@@ -336,7 +335,10 @@
             collective_id=0, has_side_effects=True, vmem_limit_bytes=2 * MIB
         ),
         name="gather",
-    )(keys, values)
+    )(
+        pltpu.with_memory_space_constraint(keys, pltpu.HBM),
+        pltpu.with_memory_space_constraint(values, pltpu.HBM),
+    )
 
     rows = tokens // 2
     wide = heads * rows

time: 39 us -> 37.3 us (0.956); the launches traced: 38.3 us -> 37 us
  local copies, waits for them, and re-layouts: 2.8 us -> 1.25 us
    unnamed x14 -> x10, local copies, waits for them, and re-layouts: 2.8 us -> 1.25 us
    pallas_call x1, Pallas kernels: 4.46 us -> 5.53 us  [shards(): pl.pallas_call(functools.partial(attend_kernel, n, heads, blocks), out_sh...]
    pallas_call x1, Pallas kernels: 13.8 us -> 12.9 us  [shards(): pl.pallas_call(functools.partial(scatter_kernel, n, head_dim ** (-0.5)),...]
where the time goes in v4:
time: 37.3 us; the launch traced here: 37 us
  Pallas kernels  35 us (94%)
  local copies, waits for them, and re-layouts  1.25 us (3%)
  between operations  0.71 us (2%)
    pallas_call x1, Pallas kernels, shards(): pl.pallas_call(functools.partial(gather_kernel, n), out_shape=pltpu.VMEM(...  16.6 us
    pallas_call x1, Pallas kernels, shards(): pl.pallas_call(functools.partial(scatter_kernel, n, head_dim ** (-0.5)),...  12.9 us
    pallas_call x1, Pallas kernels, shards(): pl.pallas_call(functools.partial(attend_kernel, n, heads, blocks), out_sh...  5.53 us
    unnamed x10, local copies, waits for them, and re-layouts  1.25 us

profile of v4, /device:TPU:0, one launch (start us, length us, event | category | flops | bytes accessed | tf_op | source)
XLA Modules:
  0.0 37.0 jit_solution(11217103215575976893)
XLA Ops:
  0.6 0.0 copy-start.3
  0.6 0.0 copy-start.2
  0.7 0.0 copy-start.1
  0.7 0.0 copy-start
  0.7 16.6 %gather.1.kv_ref = bf16[16,2,128,128]{3,2,1,0:T(8,128)(2,1)S(1)} custom-call(bf16[128,128]{1,0:T(8,128)(2,1)} %k_ref.1, bf16[128,128]{1,0:T(8,128)(2,1)} %v_ref.1), custom_call_target="tpu_custom_call" | custom-call | tf_op jit(solution)/shard_map/gather/pallas_call | solution.py:325
  17.2 0.0 copy-done.3
  17.2 0.0 copy-done.2
  17.3 0.0 copy-done.1
  17.3 0.0 copy-done
  17.3 5.5 %attend.1 = (bf16[128,1024]{1,0:T(8,128)(2,1)}, bf16[128,1024]{1,0:T(8,128)(2,1)}, bf16[16,2,128,128]{3,2,1,0:T(8,128)(2,1)S(1)}) custom-call(s32[16]{0:T(128)S(1)} %copy-done.2, s32[16]{0:T(128)S(1)} %copy-done.3, bf16[128,1024]{1,0:T(8,128)(2,1)S(1)} %copy-done, bf16[128,1024]{1,0:T(8,128)(2,1)S(1)} %copy-done.1, bf16[16,2,128,128]{3,2,1,0:T(8,128)(2,1)S(1)} %gather.1.kv_ref), custom_call_target="tpu_custom_call" | custom-call | tf_op jit(solution)/shard_map/attend/pallas_call | solution.py:347
  22.8 12.9 %scatter.1 = (bf16[128,128]{1,0:T(8,128)(2,1)S(1)}, bf16[128,128]{1,0:T(8,128)(2,1)S(1)}) custom-call(bf16[16,2,128,128]{3,2,1,0:T(8,128)(2,1)S(1)} %get-tuple-element.11.part_ref), custom_call_target="tpu_custom_call" | custom-call | tf_op jit(solution)/shard_map/scatter/pallas_call | solution.py:369
  35.7 0.6 %copy.12 = bf16[128,128]{1,0:T(8,128)(2,1)} copy(bf16[128,128]{1,0:T(8,128)(2,1)S(1)} %get-tuple-element.16) | data formatting | bytes 65536
  36.4 0.6 %copy.13 = bf16[128,128]{1,0:T(8,128)(2,1)} copy(bf16[128,128]{1,0:T(8,128)(2,1)S(1)} %get-tuple-element.17) | data formatting | bytes 65536
Async XLA Ops:
  0.6 16.6 %copy-start.3 = (s32[16]{0:T(128)S(1)}, s32[16]{0:T(128)}, u32[]{:S(2)}) copy-start(s32[16]{0:T(128)} %doc_ref.1) | copy-start | bytes 196
  0.6 16.6 %copy-start.2 = (s32[16]{0:T(128)S(1)}, s32[16]{0:T(128)}, u32[]{:S(2)}) copy-start(s32[16]{0:T(128)} %pair_ref.1) | copy-start | bytes 196
  0.7 16.6 %copy-start.1 = (bf16[128,1024]{1,0:T(8,128)(2,1)S(1)}, bf16[128,1024]{1,0:T(8,128)(2,1)}, u32[]{:S(2)}) copy-start(bf16[128,1024]{1,0:T(8,128)(2,1)} %g_ref.1) | copy-start | bytes 786436
  0.7 16.6 %copy-start = (bf16[128,1024]{1,0:T(8,128)(2,1)S(1)}, bf16[128,1024]{1,0:T(8,128)(2,1)}, u32[]{:S(2)}) copy-start(bf16[128,1024]{1,0:T(8,128)(2,1)} %q_ref.1) | copy-start | bytes 786436
